TPU v7x, 256 devices: a whole 4x4x8 slice. The times are simulated.
256 devices in a mesh: rows: 64 (over z, y, core), cols: 4 (over x).
Axes of the slice: x: 4, y: 4, z: 8, core: 2. Of those that a mesh axis runs over, the one named last changes fastest.
Arguments:
- gradients: float32 [256, 128, 4096], P(None, 'rows', 'cols'), may hold values from -6 to 6
- momentum: float32 [256, 128, 4096], P(None, 'rows', 'cols'), may hold values from -6 to 6
- weights: float32 [256, 128, 4096], P(None, 'rows', 'cols'), may hold values from -0.1875 to 0.1875
Outputs:
- new_weights: float32 [256, 128, 4096], P(None, 'rows', 'cols')
- new_momentum: float32 [256, 128, 4096], P(None, 'rows', 'cols')
All inputs are finite; a program needn't handle non-finite values.
Results may differ from a plain program's by a relative error of at most 0.0003.
Values sent between devices are 32-bit elements.
A program may use at most 64 MiB of HBM per device.

v0:
```python
import jax
import jax.numpy as jnp
from jax import lax
from jax.sharding import PartitionSpec as P

ITERS = 4


hold_rate = 0.8
learn_rate = 0.8
decay_rate = 0.1


def local(gradients, momentum, weights):
    new_momentum = hold_rate * momentum + gradients
    moved = lax.all_to_all(new_momentum, "rows", split_axis=0, concat_axis=1, tiled=True)
    whole = lax.all_to_all(moved, "cols", split_axis=0, concat_axis=2, tiled=True)
    iterate = whole * lax.rsqrt(jnp.sum(whole * whole, axis=(1, 2), keepdims=True) + 1e-06)
    for step in range(ITERS):
        gram = jnp.einsum("mik,mjk->mij", iterate, iterate, precision=lax.Precision.HIGHEST)
        mixed = -4.775 * gram + 2.0315 * jnp.einsum(
            "mij,mjk->mik", gram, gram, precision=lax.Precision.HIGHEST
        )
        iterate = 3.4445 * iterate + jnp.einsum(
            "mij,mjk->mik", mixed, iterate, precision=lax.Precision.HIGHEST
        )
    iterate = lax.all_to_all(iterate, "cols", split_axis=2, concat_axis=0, tiled=True)
    back = lax.all_to_all(iterate, "rows", split_axis=1, concat_axis=0, tiled=True)
    new_weights = (1.0 - learn_rate * decay_rate) * weights - learn_rate * back
    return (new_weights, new_momentum)


def solution(mesh):
    placed = (P(None, "rows", "cols"), P(None, "rows", "cols"), P(None, "rows", "cols"))
    return jax.shard_map(
        local,
        mesh=mesh,
        in_specs=placed,
        out_specs=(P(None, "rows", "cols"), P(None, "rows", "cols")),
        check_vma=False,
    )
```

profile of v0, /device:TPU:1, one launch (start us, length us, event | category | flops | bytes accessed | tf_op | source)
XLA Modules:
  0.0 228.9 jit_solution(2761105436010172675)
XLA Ops:
  0.6 3.7 %multiply_add_fusion = f32[256,2,1024]{2,1,0:T(2,128)S(1)} fusion(f32[256,2,1024]{2,1,0:T(2,128)} %param.3, f32[256,2,1024]{2,1,0:T(2,128)} %param.4), kind=kLoop, calls=%fused_computation.11 | loop fusion | flops 1048576 | bytes 6291456 | tf_op jit(solution)/shard_map/add | solution.py:15
  4.3 0.0 copy-start
  4.3 63.3 %all_to_all.54 = f32[256,2,1024]{2,1,0:T(2,128)S(1)} all-to-all(f32[256,2,1024]{2,1,0:T(2,128)S(1)} %multiply_add_fusion), channel_id=1, replica_groups=mesh['rows'=64,'cols'=4] {'rows'}, dimensions={0} | all-to-all | bytes 4194304 | tf_op jit(solution)/shard_map/all_to_all | solution.py:16
  67.6 0.0 copy-done
  67.6 0.8 copy.32
  68.4 2.4 %all_to_all.43 = f32[4,128,1024]{2,1,0:T(8,128)} reshape(f32[4,64,2,1024]{3,2,1,0:T(2,128)S(1)} %bitcast.56) | data formatting | bytes 4194304 | tf_op jit(solution)/shard_map/all_to_all | solution.py:16
  70.8 28.7 %all_to_all.55 = f32[4,128,1024]{2,1,0:T(8,128)S(1)} all-to-all(f32[4,128,1024]{2,1,0:T(8,128)} %all_to_all.43), channel_id=1, replica_groups=mesh['rows'=64,'cols'=4] {'cols'}, dimensions={0} | all-to-all | bytes 4194304 | tf_op jit(solution)/shard_map/all_to_all | solution.py:17
  99.5 1.1 multiply_reduce_fusion
  101.4 1.8 fusion.4
  103.2 0.2 fusion.10
  103.4 2.6 %multiply_bitcast_fusion.1 = (f32[1,128,4,1024]{3,1,2,0:T(8,128)}, f32[1,128,4,1024]{3,1,2,0:T(8,128)}) fusion(f32[4,128,1024]{2,1,0:T(8,128)S(1)} %all_to_all.55, f32[]{:T(128)S(6)} %rsqrt.4), kind=kLoop, calls=%fused_computation.13 | loop fusion | flops 1048576 | bytes 6291460 | tf_op jit(solution)/shard_map/mul | solution.py:18
  105.9 1.9 copy.26
  107.8 2.9 %copy.25 = f32[1,128,4,1024]{1,3,2,0:T(8,128)} copy(f32[1,128,4,1024]{3,1,2,0:T(8,128)} %get-tuple-element.3) | data formatting | bytes 4194304 | tf_op jit(solution)/shard_map/mul | solution.py:24
  110.7 3.0 %copy.27 = f32[128,4096]{1,0:T(8,128)} copy(f32[128,4096]{0,1:T(8,128)} %bitcast.57) | data formatting | bytes 4194304 | tf_op jit(solution)/shard_map/mul | solution.py:24
  113.7 3.6 %convolution_add_fusion.3 = f32[128,4096]{1,0:T(8,128)S(1)} fusion(f32[128,4096]{1,0:T(8,128)} %copy.27, f32[128,128]{1,0:T(8,128)S(1)} %fusion.10, f32[128,4096]{0,1:T(8,128)S(1)} %bitcast.55), kind=kOutput, calls=%fused_computation.4 | convolution fusion | flops 805830656 | bytes 6356992 | tf_op jit(solution)/shard_map/mij,mjk->mik/dot_general | solution.py:24
  117.3 1.8 fusion.12
  119.1 0.2 fusion.9
  119.3 2.0 convolution_add_fusion.2
  121.3 1.8 fusion.13
  123.1 0.2 fusion.8
  123.3 2.0 convolution_add_fusion.1
  125.4 1.8 fusion.14
  127.2 0.2 fusion.7
  127.4 2.3 fusion
  129.7 3.7 %copy.28 = f32[1,128,4096]{1,0,2:T(1,128)} copy(f32[1,128,4096]{2,1,0:T(8,128)S(1)} %fusion) | data formatting | bytes 4194304 | tf_op jit(solution)/shard_map/add | solution.py:24
  133.4 27.0 %all_to_all.56 = f32[1,128,4096]{1,0,2:T(1,128)S(1)} all-to-all(f32[1,128,4096]{1,0,2:T(1,128)} %copy.28), channel_id=1, replica_groups=mesh['rows'=64,'cols'=4] {'cols'}, dimensions={2} | all-to-all | bytes 4194304 | tf_op jit(solution)/shard_map/all_to_all | solution.py:27
  160.4 2.0 copy.29
  162.3 61.1 %all_to_all.57 = f32[4,128,1024]{2,0,1:T(4,128)S(1)} all-to-all(f32[4,128,1024]{2,0,1:T(4,128)} %bitcast.59), channel_id=1, replica_groups=mesh['rows'=64,'cols'=4] {'rows'}, dimensions={1} | all-to-all | bytes 4194304 | tf_op jit(solution)/shard_map/all_to_all | solution.py:28
  223.4 0.6 broadcast_multiply_fusion
  224.0 0.0 copy-start.1
  224.0 1.9 copy.30
  226.0 2.9 %bitcast_subtract_fusion = f32[256,2,1024]{2,1,0:T(2,128)} fusion(f32[64,4,2,1024]{3,2,1,0:T(2,128)S(1)} %copy.30, f32[256,2,1024]{2,1,0:T(2,128)S(1)} %copy-done.1), kind=kLoop, calls=%fused_computation.7 | loop fusion | flops 1048576 | bytes 6291456 | tf_op jit(solution)/shard_map/sub | solution.py:29
  (1 shorter events, 0.0 us)
Async XLA Ops:
  4.3 63.3 %copy-start = (f32[256,2,1024]{2,1,0:T(2,128)}, f32[256,2,1024]{2,1,0:T(2,128)S(1)}, u32[]{:S(2)}) copy-start(f32[256,2,1024]{2,1,0:T(2,128)S(1)} %multiply_add_fusion) | copy-start | bytes 6291460
  224.0 2.0 copy-start.1
where the time goes:
time: 230 us; the launch traced here: 229 us
  blocking collectives  180 us (78%)
  local copies, waits for them, and re-layouts  18.6 us (8%)
  matrix products  17.9 us (8%)
  other arithmetic  10.8 us (5%)
    all_to_all x1, blocking collectives, local(): lax.all_to_all(new_momentum, 'rows', split_axis=0, concat_axis=1, tiled=T...  63.3 us
    all_to_all x1, blocking collectives, local(): lax.all_to_all(iterate, 'rows', split_axis=1, concat_axis=0, tiled=True)  61.1 us
    all_to_all x1, blocking collectives, local(): lax.all_to_all(moved, 'cols', split_axis=0, concat_axis=2, tiled=True)  28.7 us
    all_to_all x1, blocking collectives, local(): lax.all_to_all(iterate, 'cols', split_axis=2, concat_axis=0, tiled=True)  27 us
    dot_general x4, matrix products, local(): jnp.einsum('mij,mjk->mik', mixed, iterate, precision=lax.Precision.HIGHEST)  9.94 us
    dot_general x4, matrix products, local(): jnp.einsum('mik,mjk->mij', iterate, iterate, precision=lax.Precision.HIGH...  7.17 us
    mul x2, local copies, waits for them, and re-layouts, local(): 3.4445 * iterate  5.84 us

commit v1 on v0

v1 whole, which is shorter than its diff:
```python
import functools

import jax
import jax.numpy as jnp
from jax import lax
from jax.experimental import pallas as pl
from jax.experimental.pallas import tpu as pltpu
from jax.sharding import PartitionSpec as P

ITERS = 4
hold_rate = 0.8
learn_rate = 0.8
decay_rate = 0.1

MESH = pl.DeviceIdType.MESH
HIGHEST = lax.Precision.HIGHEST

ROWS = 64
COLS = 4
SIDE = 128
LANES = 128
TILES = 8
PIECE = 2 * TILES
HELD = 4
STAGES = 2
PER = HELD // STAGES
BLOCK = PER * PIECE
FLAT = ROWS * HELD * PIECE
STEPS = (27, 43)


def dot(a, b, dims=(((1,), (0,)), ((), ()))):
    return lax.dot_general(a, b, dims, precision=HIGHEST, preferred_element_type=jnp.float32)


def mixing(gram):
    row = lax.broadcasted_iota(jnp.int32, (SIDE, SIDE), 0)
    col = lax.broadcasted_iota(jnp.int32, (SIDE, SIDE), 1)
    eye = row == col
    total = jnp.sum(jnp.sum(jnp.where(eye, gram, 0.0), axis=1, keepdims=True), axis=0, keepdims=True)
    scale = lax.rsqrt(total + 1e-06)
    a = gram * scale * scale
    q = None
    for step in range(ITERS):
        b = -4.775 * a + 2.0315 * dot(a, a)
        if q is None:
            q = (jnp.where(eye, 3.4445, 0.0) + b) * scale
        else:
            q = 3.4445 * q + dot(b, q)
        if step < ITERS - 1:
            half = 3.4445 * a + dot(a, b)
            a = 3.4445 * half + dot(b, half)
    return q


def kernel(
    g_hbm, m_hbm, w_hbm, nw_ref, nm_ref,
    g_buf, m_buf, w_buf, taken, spread, back, whole, part, parts, mixer,
    load_sem, in_send, in_recv, out_send, out_recv, part_send, part_recv, mix_send, mix_recv,
):
    me = lax.axis_index("rows")
    col = lax.axis_index("cols")
    z, y, core = me // 8, (me // 2) % 4, me % 2

    def peer(j, step):
        off = (j * step) % ROWS
        dz, dy, dc = off // 8, (off // 2) % 4, off % 2
        return ((z + dz) % 8) * 8 + ((y + dy) % 4) * 2 + (core + dc) % 2

    half = FLAT // 2
    loads = []
    for i, (src, dst) in enumerate(((g_hbm, g_buf), (m_hbm, m_buf), (w_hbm, w_buf))):
        load = pltpu.make_async_copy(src, dst, load_sem.at[i])
        load.start()
        loads.append(load)

    barrier = pltpu.get_barrier_semaphore()

    def greet(j, carry):
        pl.semaphore_signal(barrier, inc=1, device_id={"rows": peer(j, STEPS[0])}, device_id_type=MESH)
        return carry

    lax.fori_loop(1, ROWS, greet, 0)
    for d in range(1, COLS):
        pl.semaphore_signal(barrier, inc=1, device_id={"cols": (col + d) % COLS}, device_id_type=MESH)

    loads[0].wait()
    loads[1].wait()

    def hold(i, carry):
        at = pl.ds(pl.multiple_of(i * 64, 64), 64)
        nm_ref[at, :] = hold_rate * m_buf[at, :] + g_buf[at, :]
        return carry

    lax.fori_loop(0, FLAT // 64, hold, 0, unroll=4)

    pl.semaphore_wait(barrier, ROWS - 1 + COLS - 1)

    def block(owner, s):
        return pl.ds(pl.multiple_of(owner * (HELD * PIECE) + s * BLOCK, BLOCK), BLOCK)

    def slot(owner):
        return pl.ds(pl.multiple_of(owner * BLOCK, BLOCK), BLOCK)

    for s in range(STAGES):

        def send_in(j, carry, s=s):
            to = peer(j, STEPS[s % 2])
            pltpu.make_async_remote_copy(
                src_ref=nm_ref.at[block(to, s)],
                dst_ref=taken.at[s, slot(me)],
                send_sem=in_send.at[s],
                recv_sem=in_recv.at[s],
                device_id={"rows": to},
                device_id_type=MESH,
            ).start()
            return carry

        lax.fori_loop(1, ROWS, send_in, 0)
    for s in range(STAGES):
        taken[s, slot(me), :] = nm_ref[block(me, s), :]

    def wait_all(ref, rows, sem):
        at = ref.at[pl.ds(0, rows)]
        pltpu.make_async_copy(at, at, sem).wait()

    def grams(s):
        wait_all(taken.at[s], (ROWS - 1) * BLOCK, in_recv.at[s])
        for i in range(PER):
            k = s * PER + i
            for t in range(TILES):
                for r in range(2):
                    whole[k, pl.ds(r * ROWS, ROWS), pl.ds(t * LANES, LANES)] = taken[
                        s, pl.ds(i * PIECE + 2 * t + r, ROWS, stride=BLOCK), :
                    ]
            x = whole[k]
            gram = dot(x, x, (((1,), (1,)), ((), ())))

            @pl.when(col == k)
            def _():
                parts[k] = gram

            @pl.when(col != k)
            def _():
                part[k] = gram
                pltpu.make_async_remote_copy(
                    src_ref=part.at[k],
                    dst_ref=parts.at[col],
                    send_sem=part_send,
                    recv_sem=part_recv,
                    device_id={"cols": k},
                    device_id_type=MESH,
                ).start()

    def mix(s):
        @pl.when(col // PER == s)
        def _():
            wait_all(part, COLS - 1, part_recv)
            mixer[col] = mixing((parts[0] + parts[1]) + (parts[2] + parts[3]))
            for d in range(1, COLS):
                pltpu.make_async_remote_copy(
                    src_ref=mixer.at[col],
                    dst_ref=mixer.at[col],
                    send_sem=mix_send,
                    recv_sem=mix_recv.at[col],
                    device_id={"cols": (col + d) % COLS},
                    device_id_type=MESH,
                ).start()

    def give(s):
        for i in range(PER):
            k = s * PER + i

            @pl.when(col != k)
            def _():
                pltpu.make_async_copy(mixer.at[k], mixer.at[k], mix_recv.at[k]).wait()

            out = dot(mixer[k], whole[k])
            for t in range(TILES):
                for r in range(2):
                    spread[s, pl.ds(i * PIECE + 2 * t + r, ROWS, stride=BLOCK), :] = out[
                        r * ROWS : (r + 1) * ROWS, t * LANES : (t + 1) * LANES
                    ]

        def send_out(j, carry):
            to = peer(j, STEPS[s % 2])
            pltpu.make_async_remote_copy(
                src_ref=spread.at[s, slot(to)],
                dst_ref=back.at[block(me, s)],
                send_sem=out_send.at[s],
                recv_sem=out_recv.at[s],
                device_id={"rows": to},
                device_id_type=MESH,
            ).start()
            return carry

        lax.fori_loop(1, ROWS, send_out, 0)
        back[block(me, s), :] = spread[s, slot(me), :]

    for s in range(STAGES):
        grams(s)
        mix(s)
        if s:
            give(s - 1)
    give(STAGES - 1)

    loads[2].wait()
    for s in range(STAGES):
        wait_all(back, (ROWS - 1) * BLOCK, out_recv.at[s])

        def decay(r, carry, s=s):
            at = block(r, s)
            nw_ref[at, :] = (1.0 - learn_rate * decay_rate) * w_buf[at, :] - learn_rate * back[at, :]
            return carry

        lax.fori_loop(0, ROWS, decay, 0, unroll=4)

    for s in range(STAGES):
        wait_all(back, (ROWS - 1) * BLOCK, in_send.at[s])
        wait_all(back, (ROWS - 1) * BLOCK, out_send.at[s])
    wait_all(part, COLS - 1, part_send)
    wait_all(part, COLS - 1, mix_send)


def flat(a):
    return a.reshape(ROWS * HELD, 2, TILES, LANES).transpose(0, 2, 1, 3).reshape(FLAT, LANES)


def square(a):
    return a.reshape(ROWS * HELD, TILES, 2, LANES).transpose(0, 2, 1, 3).reshape(ROWS * HELD, 2, TILES * LANES)


def local(gradients, momentum, weights):
    f32 = jnp.float32
    in_hbm = [pltpu.with_memory_space_constraint(flat(a), pltpu.HBM) for a in (gradients, momentum, weights)]
    vmem = pltpu.VMEM
    dma = pltpu.SemaphoreType.DMA
    new_weights, new_momentum = pl.pallas_call(
        kernel,
        out_shape=[pltpu.VMEM((FLAT, LANES), f32)] * 2,
        in_specs=[pl.BlockSpec(memory_space=pltpu.HBM)] * 3,
        scratch_shapes=[
            vmem((FLAT, LANES), f32),
            vmem((FLAT, LANES), f32),
            vmem((FLAT, LANES), f32),
            vmem((STAGES, ROWS * BLOCK, LANES), f32),
            vmem((STAGES, ROWS * BLOCK, LANES), f32),
            vmem((FLAT, LANES), f32),
            vmem((HELD, SIDE, TILES * LANES), f32),
            vmem((HELD, SIDE, SIDE), f32),
            vmem((COLS, SIDE, SIDE), f32),
            vmem((HELD, SIDE, SIDE), f32),
            dma((3,)),
            dma((STAGES,)),
            dma((STAGES,)),
            dma((STAGES,)),
            dma((STAGES,)),
            dma(()),
            dma(()),
            dma(()),
            dma((HELD,)),
        ],
        compiler_params=pltpu.CompilerParams(
            collective_id=0, has_side_effects=True, vmem_limit_bytes=40 * 2**20
        ),
        name="step",
    )(*in_hbm)
    return square(new_weights), square(new_momentum)


def solution(mesh):
    placed = P(None, "rows", "cols")
    return jax.shard_map(
        local, mesh=mesh, in_specs=(placed, placed, placed), out_specs=(placed, placed), check_vma=False
    )
```

time: 230 us -> 125 us (0.54)
  the two profiles are of different devices: /device:TPU:1 before, /device:TPU:39 now
where the time goes in v1:
time: 125 us
  Pallas kernels  122 us (98%)
  local copies, waits for them, and re-layouts  2.64 us (2%)
    pallas_call x1, Pallas kernels, local(): pl.pallas_call(kernel, out_shape=[pltpu.VMEM((FLAT, LANES), f32)] * 2, in...  122 us
    unnamed x2, local copies, waits for them, and re-layouts  2.64 us

profile of v1, /device:TPU:39, one launch (start us, length us, event | category | flops | bytes accessed | tf_op | source)
XLA Modules:
  0.0 124.9 jit_solution(5426917360012417378)
XLA Ops:
  0.6 121.6 %step.1 = (f32[4096,128]{1,0:T(8,128)S(1)}, f32[4096,128]{1,0:T(8,128)S(1)}) custom-call(f32[4096,128]{1,0:T(8,128)} %bitcast.27, f32[4096,128]{1,0:T(8,128)} %bitcast.28, f32[4096,128]{1,0:T(8,128)} %bitcast.29), custom_call_target="tpu_custom_call" | custom-call | tf_op jit(solution)/shard_map/step/pallas_call | solution.py:238
  122.2 1.3 %copy.12 = f32[256,2,1024]{2,1,0:T(2,128)} copy(f32[256,2,1024]{2,1,0:T(2,128)S(1)} %bitcast.26) | data formatting | bytes 4194304
  123.5 1.3 %copy.13 = f32[256,2,1024]{2,1,0:T(2,128)} copy(f32[256,2,1024]{2,1,0:T(2,128)S(1)} %bitcast.25) | data formatting | bytes 4194304

commit v2 on v1

--- a/solution.py
+++ b/solution.py
@@ -22,7 +22,7 @@
 TILES = 8
 PIECE = 2 * TILES
 HELD = 4
-STAGES = 2
+STAGES = 4
 PER = HELD // STAGES
 BLOCK = PER * PIECE
 FLAT = ROWS * HELD * PIECE
@@ -200,9 +200,7 @@
     for s in range(STAGES):
         grams(s)
         mix(s)
-        if s:
-            give(s - 1)
-    give(STAGES - 1)
+        give(s)
 
     loads[2].wait()
     for s in range(STAGES):

time: 125 us -> 110 us (0.88)
  the two profiles are of different devices: /device:TPU:39 before, /device:TPU:1 now
where the time goes in v2:
time: 110 us
  Pallas kernels  107 us (97%)
  local copies, waits for them, and re-layouts  2.64 us (2%)
    pallas_call x1, Pallas kernels, local(): pl.pallas_call(kernel, out_shape=[pltpu.VMEM((FLAT, LANES), f32)] * 2, in...  107 us
    unnamed x2, local copies, waits for them, and re-layouts  2.64 us

profile of v2, /device:TPU:1, one launch (start us, length us, event | category | flops | bytes accessed | tf_op | source)
XLA Modules:
  0.0 110.1 jit_solution(15143712197259034512)
XLA Ops:
  0.6 106.8 %step.1 = (f32[4096,128]{1,0:T(8,128)S(1)}, f32[4096,128]{1,0:T(8,128)S(1)}) custom-call(f32[4096,128]{1,0:T(8,128)} %bitcast.27, f32[4096,128]{1,0:T(8,128)} %bitcast.28, f32[4096,128]{1,0:T(8,128)} %bitcast.29), custom_call_target="tpu_custom_call" | custom-call | tf_op jit(solution)/shard_map/step/pallas_call | solution.py:236
  107.4 1.3 %copy.12 = f32[256,2,1024]{2,1,0:T(2,128)} copy(f32[256,2,1024]{2,1,0:T(2,128)S(1)} %bitcast.26) | data formatting | bytes 4194304
  108.8 1.3 %copy.13 = f32[256,2,1024]{2,1,0:T(2,128)} copy(f32[256,2,1024]{2,1,0:T(2,128)S(1)} %bitcast.25) | data formatting | bytes 4194304

commit v3 on v2

--- a/solution.py
+++ b/solution.py
@@ -15,7 +15,9 @@
 MESH = pl.DeviceIdType.MESH
 HIGHEST = lax.Precision.HIGHEST
 
-ROWS = 64
+DEPTH = 8
+PLANE = 8
+ROWS = DEPTH * PLANE
 COLS = 4
 SIDE = 128
 LANES = 128
@@ -56,7 +58,7 @@
 def kernel(
     g_hbm, m_hbm, w_hbm, nw_ref, nm_ref,
     g_buf, m_buf, w_buf, taken, spread, back, whole, part, parts, mixer,
-    load_sem, in_send, in_recv, out_send, out_recv, part_send, part_recv, mix_send, mix_recv,
+    load_sem, in_send, in_recv, out_send, out_recv, part_send, part_recv, mix_send, mix_recv, below, above,
 ):
     me = lax.axis_index("rows")
     col = lax.axis_index("cols")
@@ -76,11 +78,21 @@
 
     barrier = pltpu.get_barrier_semaphore()
 
-    def greet(j, carry):
-        pl.semaphore_signal(barrier, inc=1, device_id={"rows": peer(j, STEPS[0])}, device_id_type=MESH)
-        return carry
-
-    lax.fori_loop(1, ROWS, greet, 0)
+    def away(dz, j):
+        return ((z + dz) % DEPTH) * PLANE + (me + j) % PLANE
+
+    def greet(dz, j):
+        pl.semaphore_signal(barrier, inc=1, device_id={"rows": away(dz, j)}, device_id_type=MESH)
+
+    @pl.loop(0, PLANE)
+    def _(j):
+        greet(DEPTH - 1, j)
+        greet(1, j)
+
+    @pl.loop(1, PLANE)
+    def _(j):
+        greet(0, j)
+
     for d in range(1, COLS):
         pl.semaphore_signal(barrier, inc=1, device_id={"cols": (col + d) % COLS}, device_id_type=MESH)
 
@@ -94,7 +106,17 @@
 
     lax.fori_loop(0, FLAT // 64, hold, 0, unroll=4)
 
-    pl.semaphore_wait(barrier, ROWS - 1 + COLS - 1)
+    pl.semaphore_wait(barrier, 3 * PLANE - 1 + COLS - 1)
+
+    def tell():
+        pl.semaphore_signal(below, inc=1, device_id={"rows": away(1, 0)}, device_id_type=MESH)
+        pl.semaphore_signal(above, inc=1, device_id={"rows": away(DEPTH - 1, 0)}, device_id_type=MESH)
+
+    def hear():
+        pl.semaphore_wait(below, 1)
+        pl.semaphore_wait(above, 1)
+
+    tell()
 
     def block(owner, s):
         return pl.ds(pl.multiple_of(owner * (HELD * PIECE) + s * BLOCK, BLOCK), BLOCK)
@@ -102,21 +124,40 @@
     def slot(owner):
         return pl.ds(pl.multiple_of(owner * BLOCK, BLOCK), BLOCK)
 
-    for s in range(STAGES):
-
-        def send_in(j, carry, s=s):
-            to = peer(j, STEPS[s % 2])
-            pltpu.make_async_remote_copy(
-                src_ref=nm_ref.at[block(to, s)],
-                dst_ref=taken.at[s, slot(me)],
-                send_sem=in_send.at[s],
-                recv_sem=in_recv.at[s],
-                device_id={"rows": to},
-                device_id_type=MESH,
-            ).start()
-            return carry
-
-        lax.fori_loop(1, ROWS, send_in, 0)
+    def send_in(to, s):
+        pltpu.make_async_remote_copy(
+            src_ref=nm_ref.at[block(to, s)],
+            dst_ref=taken.at[s, slot(me)],
+            send_sem=in_send.at[s],
+            recv_sem=in_recv.at[s],
+            device_id={"rows": to},
+            device_id_type=MESH,
+        ).start()
+
+    for dz in range(1, DEPTH // 2 + 1):
+        if dz > 1:
+            hear()
+            if dz < DEPTH // 2:
+                tell()
+
+        @pl.loop(0, PLANE)
+        def _(j, dz=dz):
+            send_in(away(dz, j), 0)
+            if dz < DEPTH // 2:
+                send_in(away(DEPTH - dz, j), 0)
+
+        if dz == 1:
+
+            @pl.loop(1, PLANE)
+            def _(j):
+                send_in(away(0, j), 0)
+
+    for s in range(1, STAGES):
+
+        @pl.loop(1, ROWS)
+        def _(j, s=s):
+            send_in(peer(j, STEPS[s % 2]), s)
+
     for s in range(STAGES):
         taken[s, slot(me), :] = nm_ref[block(me, s), :]
 
@@ -218,6 +259,17 @@
         wait_all(back, (ROWS - 1) * BLOCK, out_send.at[s])
     wait_all(part, COLS - 1, part_send)
     wait_all(part, COLS - 1, mix_send)
+
+
+def store(nw_ref, nm_ref, nw_hbm, nm_hbm, sem):
+    copies = [
+        pltpu.make_async_copy(nw_ref, nw_hbm, sem.at[0]),
+        pltpu.make_async_copy(nm_ref, nm_hbm, sem.at[1]),
+    ]
+    for copy in copies:
+        copy.start()
+    for copy in copies:
+        copy.wait()
 
 
 def flat(a):
@@ -257,12 +309,23 @@
             dma(()),
             dma(()),
             dma((HELD,)),
+            pltpu.SemaphoreType.REGULAR,
+            pltpu.SemaphoreType.REGULAR,
         ],
         compiler_params=pltpu.CompilerParams(
             collective_id=0, has_side_effects=True, vmem_limit_bytes=40 * 2**20
         ),
         name="step",
     )(*in_hbm)
+    new_weights, new_momentum = pl.pallas_call(
+        store,
+        out_shape=[jax.ShapeDtypeStruct((FLAT, LANES), f32)] * 2,
+        in_specs=[pl.BlockSpec(memory_space=pltpu.VMEM)] * 2,
+        out_specs=[pl.BlockSpec(memory_space=pl.ANY)] * 2,
+        scratch_shapes=[dma((2,))],
+        compiler_params=pltpu.CompilerParams(vmem_limit_bytes=2**20),
+        name="store",
+    )(new_weights, new_momentum)
     return square(new_weights), square(new_momentum)
 
 

time: 110 us -> 108 us (0.982)
  local copies, waits for them, and re-layouts: 2.64 us -> 0 us
    unnamed x2 -> x0, local copies, waits for them, and re-layouts: 2.64 us -> none
    pallas_call x0 -> x1, Pallas kernels: none -> 2.03 us  [local(): pl.pallas_call(store, out_shape=[jax.ShapeDtypeStruct((FLAT, LANES), f32)...]
    pallas_call x1, Pallas kernels: 107 us -> 105 us  [local(): pl.pallas_call(kernel, out_shape=[pltpu.VMEM((FLAT, LANES), f32)] * 2, in...]
where the time goes in v3:
time: 108 us
  Pallas kernels  107 us (99%)
    pallas_call x1, Pallas kernels, local(): pl.pallas_call(kernel, out_shape=[pltpu.VMEM((FLAT, LANES), f32)] * 2, in...  105 us

profile of v3, /device:TPU:1, one launch (start us, length us, event | category | flops | bytes accessed | tf_op | source)
XLA Modules:
  0.0 107.8 jit_solution(18374215218814241378)
XLA Ops:
  0.6 105.1 %step.1 = (f32[4096,128]{1,0:T(8,128)S(1)}, f32[4096,128]{1,0:T(8,128)S(1)}) custom-call(f32[4096,128]{1,0:T(8,128)} %bitcast.25, f32[4096,128]{1,0:T(8,128)} %bitcast.26, f32[4096,128]{1,0:T(8,128)} %bitcast.27), custom_call_target="tpu_custom_call" | custom-call | tf_op jit(solution)/shard_map/step/pallas_call | solution.py:288
  105.7 2.0 %store.1 = (f32[4096,128]{1,0:T(8,128)}, f32[4096,128]{1,0:T(8,128)}) custom-call(f32[4096,128]{1,0:T(8,128)S(1)} %get-tuple-element.6.nw_ref, f32[4096,128]{1,0:T(8,128)S(1)} %get-tuple-element.7.nm_ref), custom_call_target="tpu_custom_call" | custom-call | tf_op jit(solution)/shard_map/store/pallas_call | solution.py:320

commit v4 on v3

--- a/solution.py
+++ b/solution.py
@@ -28,7 +28,7 @@
 PER = HELD // STAGES
 BLOCK = PER * PIECE
 FLAT = ROWS * HELD * PIECE
-STEPS = (27, 43)
+STEPS = (13, 37)
 
 
 def dot(a, b, dims=(((1,), (0,)), ((), ()))):
@@ -81,6 +81,19 @@
     def away(dz, j):
         return ((z + dz) % DEPTH) * PLANE + (me + j) % PLANE
 
+    def far_first(send):
+        for dz in range(DEPTH // 2, 0, -1):
+
+            @pl.loop(0, PLANE)
+            def _(j, dz=dz):
+                send(away(dz, j))
+                if dz < DEPTH // 2:
+                    send(away(DEPTH - dz, j))
+
+        @pl.loop(1, PLANE)
+        def _(j):
+            send(away(0, j))
+
     def greet(dz, j):
         pl.semaphore_signal(barrier, inc=1, device_id={"rows": away(dz, j)}, device_id_type=MESH)
 
@@ -223,8 +236,7 @@
                         r * ROWS : (r + 1) * ROWS, t * LANES : (t + 1) * LANES
                     ]
 
-        def send_out(j, carry):
-            to = peer(j, STEPS[s % 2])
+        def send_out(to):
             pltpu.make_async_remote_copy(
                 src_ref=spread.at[s, slot(to)],
                 dst_ref=back.at[block(me, s)],
@@ -233,9 +245,15 @@
                 device_id={"rows": to},
                 device_id_type=MESH,
             ).start()
-            return carry
-
-        lax.fori_loop(1, ROWS, send_out, 0)
+
+        if s < 3:
+
+            @pl.loop(1, ROWS)
+            def _(j):
+                send_out(peer(j, STEPS[s % 2]))
+        else:
+            far_first(send_out)
+
         back[block(me, s), :] = spread[s, slot(me), :]
 
     for s in range(STAGES):

time: 108 us -> 107 us (level)
  no operation moved by 1% of the time
where the time goes in v4:
time: 107 us
  Pallas kernels  106 us (99%)
    pallas_call x1, Pallas kernels, local(): pl.pallas_call(kernel, out_shape=[pltpu.VMEM((FLAT, LANES), f32)] * 2, in...  104 us

profile of v4, /device:TPU:1, one launch (start us, length us, event | category | flops | bytes accessed | tf_op | source)
XLA Modules:
  0.0 106.8 jit_solution(11631739613663504544)
XLA Ops:
  0.6 104.2 %step.1 = (f32[4096,128]{1,0:T(8,128)S(1)}, f32[4096,128]{1,0:T(8,128)S(1)}) custom-call(f32[4096,128]{1,0:T(8,128)} %bitcast.25, f32[4096,128]{1,0:T(8,128)} %bitcast.26, f32[4096,128]{1,0:T(8,128)} %bitcast.27), custom_call_target="tpu_custom_call" | custom-call | tf_op jit(solution)/shard_map/step/pallas_call | solution.py:306
  104.8 2.0 %store.1 = (f32[4096,128]{1,0:T(8,128)}, f32[4096,128]{1,0:T(8,128)}) custom-call(f32[4096,128]{1,0:T(8,128)S(1)} %get-tuple-element.6.nw_ref, f32[4096,128]{1,0:T(8,128)S(1)} %get-tuple-element.7.nm_ref), custom_call_target="tpu_custom_call" | custom-call | tf_op jit(solution)/shard_map/store/pallas_call | solution.py:338

commit v5 on v3

--- a/solution.py
+++ b/solution.py
@@ -28,7 +28,7 @@
 PER = HELD // STAGES
 BLOCK = PER * PIECE
 FLAT = ROWS * HELD * PIECE
-STEPS = (27, 43)
+STEPS = (13, 37)
 
 
 def dot(a, b, dims=(((1,), (0,)), ((), ()))):
@@ -223,8 +223,7 @@
                         r * ROWS : (r + 1) * ROWS, t * LANES : (t + 1) * LANES
                     ]
 
-        def send_out(j, carry):
-            to = peer(j, STEPS[s % 2])
+        def send_out(to):
             pltpu.make_async_remote_copy(
                 src_ref=spread.at[s, slot(to)],
                 dst_ref=back.at[block(me, s)],
@@ -233,9 +232,24 @@
                 device_id={"rows": to},
                 device_id_type=MESH,
             ).start()
-            return carry
-
-        lax.fori_loop(1, ROWS, send_out, 0)
+
+        if s < STAGES - 1:
+
+            @pl.loop(1, ROWS)
+            def _(j):
+                send_out(peer(j, STEPS[s % 2]))
+        else:
+            for planes in ((0, 1), (2, 3, 4, 5, 6, 7)):
+
+                @pl.loop(0, PLANE)
+                def _(j, planes=planes):
+                    for plane in planes:
+                        to = plane * PLANE + (me + j) % PLANE
+
+                        @pl.when(to != me)
+                        def _(to=to):
+                            send_out(to)
+
         back[block(me, s), :] = spread[s, slot(me), :]
 
     for s in range(STAGES):

time: 108 us -> 105 us (0.972)
  Pallas kernels: 107 us -> 104 us
    pallas_call x1, Pallas kernels: 105 us -> 102 us  [local(): pl.pallas_call(kernel, out_shape=[pltpu.VMEM((FLAT, LANES), f32)] * 2, in...]
where the time goes in v5:
time: 105 us
  Pallas kernels  104 us (99%)
    pallas_call x1, Pallas kernels, local(): pl.pallas_call(kernel, out_shape=[pltpu.VMEM((FLAT, LANES), f32)] * 2, in...  102 us

profile of v5, /device:TPU:1, one launch (start us, length us, event | category | flops | bytes accessed | tf_op | source)
XLA Modules:
  0.0 104.6 jit_solution(15530254882246983598)
XLA Ops:
  0.6 102.0 %step.1 = (f32[4096,128]{1,0:T(8,128)S(1)}, f32[4096,128]{1,0:T(8,128)S(1)}) custom-call(f32[4096,128]{1,0:T(8,128)} %bitcast.25, f32[4096,128]{1,0:T(8,128)} %bitcast.26, f32[4096,128]{1,0:T(8,128)} %bitcast.27), custom_call_target="tpu_custom_call" | custom-call | tf_op jit(solution)/shard_map/step/pallas_call | solution.py:302
  102.6 2.0 %store.1 = (f32[4096,128]{1,0:T(8,128)}, f32[4096,128]{1,0:T(8,128)}) custom-call(f32[4096,128]{1,0:T(8,128)S(1)} %get-tuple-element.6.nw_ref, f32[4096,128]{1,0:T(8,128)S(1)} %get-tuple-element.7.nm_ref), custom_call_target="tpu_custom_call" | custom-call | tf_op jit(solution)/shard_map/store/pallas_call | solution.py:334

commit v6 on v5

--- a/solution.py
+++ b/solution.py
@@ -239,7 +239,7 @@
             def _(j):
                 send_out(peer(j, STEPS[s % 2]))
         else:
-            for planes in ((0, 1), (2, 3, 4, 5, 6, 7)):
+            for planes in ((0, 1), (2, 3, 7), (4, 5, 6)):
 
                 @pl.loop(0, PLANE)
                 def _(j, planes=planes):

time: 105 us -> 106 us (level); the launches traced: 105 us -> 104 us
  no operation moved by 1% of the time
where the time goes in v6:
time: 106 us; the launch traced here: 104 us
  Pallas kernels  103 us (97%)
    pallas_call x1, Pallas kernels, local(): pl.pallas_call(kernel, out_shape=[pltpu.VMEM((FLAT, LANES), f32)] * 2, in...  101 us

profile of v6, /device:TPU:1, one launch (start us, length us, event | category | flops | bytes accessed | tf_op | source)
XLA Modules:
  0.0 104.1 jit_solution(12685913894053445907)
XLA Ops:
  0.6 101.4 %step.1 = (f32[4096,128]{1,0:T(8,128)S(1)}, f32[4096,128]{1,0:T(8,128)S(1)}) custom-call(f32[4096,128]{1,0:T(8,128)} %bitcast.25, f32[4096,128]{1,0:T(8,128)} %bitcast.26, f32[4096,128]{1,0:T(8,128)} %bitcast.27), custom_call_target="tpu_custom_call" | custom-call | tf_op jit(solution)/shard_map/step/pallas_call | solution.py:302
  102.1 2.0 %store.1 = (f32[4096,128]{1,0:T(8,128)}, f32[4096,128]{1,0:T(8,128)}) custom-call(f32[4096,128]{1,0:T(8,128)S(1)} %get-tuple-element.6.nw_ref, f32[4096,128]{1,0:T(8,128)S(1)} %get-tuple-element.7.nm_ref), custom_call_target="tpu_custom_call" | custom-call | tf_op jit(solution)/shard_map/store/pallas_call | solution.py:334
